TPU v7x, 32 devices: a whole 2x2x4 slice. The times are simulated.
32 devices in a mesh: tm: 8 (over y, x, core), space: 4 (over z).
Axes of the slice: x: 2, y: 2, z: 4, core: 2. Of those that a mesh axis runs over, the one named last changes fastest.
Arguments:
- speed: float32 [8, 16, 128], P('space'), may hold values from 0.5 to 1.5
- forcing: float32 [32, 8, 16, 128], P('tm', 'space'), may hold values from -1.8 to 1.8
- guess: float32 [8, 4, 8, 16, 128], P('tm', None, 'space'), may hold values from -8 to 8
- basis: float32 [8, 64, 4, 8, 16, 128], P('tm', None, None, 'space'), may hold values from -1 to 1, as said below
Outputs:
- states: float32 [32, 4, 8, 16, 128], P('tm', None, 'space')
- coords: float32 [8, 64], P('tm')
Inputs may be any that keep to these rules, and one draw needn't show every extreme that they name: The columns of each basis[k] are linearly independent.
All inputs are finite; a program needn't handle non-finite values.
Results may differ from a plain program's by a relative error of at most 0.00018.
Values sent between devices are 32-bit elements; how exact they have to be, the bound alone decides.
A program may use at most 128 MiB of HBM per device.

v0:
```python
import jax
import jax.numpy as jnp
from jax import lax
from jax.experimental import pallas as pl
from jax.experimental.pallas import tpu as pltpu
from jax.sharding import PartitionSpec as P

DT = 0.045
GROUP = 4
MESH = pl.DeviceIdType.MESH


def phi(state, speed_sq, h):
    p, vx, vy, vz = state
    nx, ny = p.shape[1], p.shape[2]
    row = lax.broadcasted_iota(jnp.int32, p.shape, 1)
    lane = lax.broadcasted_iota(jnp.int32, p.shape, 2)
    zero = jnp.zeros_like(p[:1])
    px = jnp.where(row == nx - 1, 0.0, pltpu.roll(p, nx - 1, 1))
    py = jnp.where(lane == ny - 1, 0.0, pltpu.roll(p, ny - 1, 2))
    pz = jnp.concatenate([p[1:], zero], axis=0)
    vx = vx - h * (px - p)
    vy = vy - h * (py - p)
    vz = vz - h * (pz - p)
    bx = jnp.where(row == 0, 0.0, pltpu.roll(vx, 1, 1))
    by = jnp.where(lane == 0, 0.0, pltpu.roll(vy, 1, 2))
    bz = jnp.concatenate([zero, vz[:-1]], axis=0)
    p = p - h * speed_sq * ((vx - bx) + (vy - by) + (vz - bz))
    return (p, vx, vy, vz)


def make_kernel(n_tm, n_sp, rank, slab):
    n_chain = n_tm // GROUP - 1

    def kernel(
        speed_in, forcing_in, guess_in, basis_in, states_out, coords_out,
        speed, forcing, basis, rx, tx, ys, cf, gb, inv, acc, wb,
        local_sem, send_sems, recv_sems,
    ):
        k = lax.axis_index("tm")
        s = lax.axis_index("space")
        nxt = lax.rem(k + 1, n_tm)
        mine = pl.ds(slab * s, slab)

        def peer(d):
            return lax.rem(s + d, n_sp)

        copies = [
            pltpu.make_async_copy(speed_in, speed.at[:, mine], local_sem.at[1]),
            pltpu.make_async_copy(forcing_in, forcing.at[:, mine], local_sem.at[2]),
            pltpu.make_async_copy(basis_in, basis, local_sem.at[3]),
        ]
        for c in copies:
            c.start()

        before = lax.rem(k + n_tm - 1, n_tm)
        partners = [(k, peer(d)) for d in range(1, n_sp)]
        groups = [nxt, before]
        for j in range(1, n_chain + 1):
            groups.append(lax.rem(k + 1 + GROUP * j, n_tm))
            groups.append(lax.rem(k + n_tm - 1 - GROUP * j, n_tm))
        for group in groups:
            partners += [(group, peer(d)) for d in range(n_sp)]
        barrier = pltpu.get_barrier_semaphore()
        for target in partners:
            pl.semaphore_signal(barrier, inc=1, device_id=target, device_id_type=MESH)
        pl.semaphore_wait(barrier, len(partners))

        sent = []

        class Remote:
            def __init__(self, src, dst, target, sends=None, receives=None):
                i = len(sent)
                self.copy = pltpu.make_async_remote_copy(
                    src_ref=src, dst_ref=dst, send_sem=send_sems.at[i], recv_sem=recv_sems.at[i],
                    device_id=target, device_id_type=MESH,
                )
                self.sends, self.receives = sends, receives
                sent.append(self)
                self.under(sends, self.copy.start)

            def under(self, condition, act):
                if condition is None:
                    act()
                else:
                    pl.when(condition)(act)

            def wait_recv(self):
                self.under(self.receives, self.copy.wait_recv)

            def wait_send(self):
                self.under(self.sends, self.copy.wait_send)

        def remote(src, dst, target):
            return Remote(src, dst, target)

        def inside(at):
            return (at >= 0) & (at < n_sp)

        def spread(src, base, dst, group, pieces):
            made = []
            for delta, comps, offset, planes in pieces:
                made.append(Remote(
                    src.at[comps, pl.ds(base + offset, planes)],
                    dst.at[comps, pl.ds(slab * s + offset, planes)],
                    (group, s + delta),
                    None if delta == 0 else inside(s + delta),
                    None if delta == 0 else inside(s - delta),
                ))
            return made

        def state_pieces(reach):
            pieces = []
            delta = 1
            while reach - (delta - 1) * slab > 0:
                left = reach - (delta - 1) * slab
                near = min(slab, left - 1)
                if near:
                    pieces.append((delta, slice(0, 4), slab - near, near))
                    pieces.append((-delta, slice(0, 4), 0, near))
                if left <= slab:
                    pieces.append((delta, slice(0, 1), slab - left, 1))
                    pieces.append((delta, slice(3, 4), slab - left, 1))
                    pieces.append((-delta, slice(0, 1), left - 1, 1))
                delta += 1
            return pieces[::-1]

        own = [(0, slice(0, 4), 0, slab)]

        def load_pieces(reach):
            pieces = []
            delta = 1
            while reach - (delta - 1) * slab > 0:
                left = reach - (delta - 1) * slab
                planes = min(slab, left)
                pieces.append((delta, slice(0, left), slab - planes, planes))
                pieces.append((-delta, slice(0, left), 0, planes))
                delta += 1
            return pieces[::-1]

        first = spread(guess_in, 0, rx.at[0], nxt, state_pieces(4) + own)
        first += spread(forcing_in, 0, forcing, k, load_pieces(3))
        first += spread(speed_in, 0, speed, k, [(d, slice(0, 1), o, n) for d, c, o, n in load_pieces(3)])

        def load(ref):
            return tuple(ref[i] for i in range(4))

        def store(ref, state):
            for i in range(4):
                ref[i] = state[i]

        def fine(i, state):
            p, vx, vy, vz = phi(state, speed[0] * speed[0], DT)
            return (p + forcing[i], vx, vy, vz)

        def plain(i, state):
            return phi(state, speed[0] * speed[0], DT)

        def shift(index, src, group, reach):
            pieces = own + state_pieces(1) if reach == 1 else state_pieces(reach) + own
            return spread(src, slab * s, rx.at[index], group, pieces)

        copies[2].wait()

        def gram_step(i, total):
            t = jnp.swapaxes(basis[:, i], 0, 1)
            hi = t.astype(jnp.bfloat16)
            rest = t - hi.astype(jnp.float32)
            mid = rest.astype(jnp.bfloat16)
            low = (rest - mid.astype(jnp.float32)).astype(jnp.bfloat16)
            parts = jnp.concatenate([hi, mid, low], axis=1)
            flat = jnp.concatenate([parts[j] for j in range(parts.shape[0])], axis=1)
            return total + lax.dot_general(
                flat, flat, (((1,), (1,)), ((), ())), preferred_element_type=jnp.float32
            )

        full = lax.fori_loop(0, basis.shape[1], gram_step, jnp.zeros((3 * rank, 3 * rank), jnp.float32))
        hh, hm, hl = full[:rank, :rank], full[:rank, rank:2 * rank], full[:rank, 2 * rank:]
        mh, mm, lh = full[rank:2 * rank, :rank], full[rank:2 * rank, rank:2 * rank], full[2 * rank:, :rank]
        gram = hh + ((hm + mh) + (mm + (hl + lh)))
        gb[s] = jnp.concatenate([gram, jnp.zeros_like(gram)], axis=1)
        gram_copies = [remote(gb.at[s], gb.at[s], (k, peer(d))) for d in range(1, n_sp)]

        copies[0].wait()
        copies[1].wait()
        for c in first:
            c.wait_recv()
        state = lax.fori_loop(0, 4, fine, load(rx.at[0]))
        store(tx.at[0], state)
        moved = shift(1, tx.at[0], nxt, 4)

        for c in gram_copies:
            c.wait_recv()
        g = gb[0]
        for i in range(1, n_sp):
            g = g + gb[i]
        rows = lax.broadcasted_iota(jnp.int32, g.shape, 0)
        lanes = lax.broadcasted_iota(jnp.int32, g.shape, 1)
        m = jnp.where(lanes == rows + rank, 1.0, g)
        for j in range(rank):
            pivot = m[j:j + 1]
            pivot = pivot / pivot[:, j:j + 1]
            m = jnp.where(rows == j, pivot, m - m[:, j:j + 1] * pivot)
        inverse = m[:, rank:]
        inv[...] = jnp.concatenate([inverse, jnp.zeros_like(inverse)], axis=1)
        acc[rank:, :] = jnp.zeros((rank, acc.shape[1]), jnp.float32)

        for c in moved:
            c.wait_recv()
        state = lax.fori_loop(0, 4, fine, load(rx.at[1]))
        residue = tx.at[1]
        for i in range(4):
            residue[i] = state[i] - tx[0, i]

        def weights(index, x):
            def coef_step(i, carry):
                b = basis[pl.ds(8 * i, 8)]
                t = jnp.sum(b * x[None], axis=1)
                half = t.shape[1] // 2
                t = t[:, :half] + t[:, half:]
                acc[pl.ds(pl.multiple_of(8 * i, 8), 8), :] = jnp.sum(t, axis=1)
                return carry

            lax.fori_loop(0, rank // 8, coef_step, 0)
            ones = jnp.ones((8, acc.shape[1]), jnp.float32)
            cf[index, s] = lax.dot_general(
                ones, acc[...], (((1,), (1,)), ((), ())),
                precision=lax.Precision.HIGHEST, preferred_element_type=jnp.float32,
            )
            made = [
                remote(cf.at[index, s], cf.at[index, s], (k, peer(d)))
                for d in range(1, n_sp)
            ]
            return made

        def solve(index, made):
            for c in made:
                c.wait_recv()
            total = cf[index, 0]
            for i in range(1, n_sp):
                total = total + cf[index, i]
            w = jnp.sum(inv[...] * total[:1], axis=1, keepdims=True)
            return jnp.broadcast_to(w, wb.shape)

        def slab_of(ref):
            x = ref[:, mine]
            return x.reshape((x.shape[0] * x.shape[1],) + x.shape[2:])

        def candidate(index, x_ref, late):
            wb[...] = solve(index, weights(index, slab_of(x_ref)))

            def sum_step(r, y):
                return y + wb[pl.ds(r, 1), :][None] * basis[r]

            y = lax.fori_loop(0, rank, sum_step, jnp.zeros(basis.shape[1:], jnp.float32), unroll=4)
            ys[index, :, mine] = y.reshape((4, slab) + y.shape[1:])
            made = spread(ys.at[index], slab * s, ys.at[index], k, state_pieces(4))
            for c in late + made:
                c.wait_recv()
            ally = load(ys.at[index])
            ahead = phi(tuple(x_ref[i] - ally[i] for i in range(4)), speed[0] * speed[0], 4 * DT)
            for i in range(4):
                acc4[i] = ahead[i] + residue[i]
            corrected = lax.fori_loop(0, 4, plain, load(ys.at[index]))
            return tuple(corrected[i] + acc4[i] for i in range(4))

        acc4 = tx.at[6]

        moved = shift(2, residue, nxt, 1)
        for index in range(3):
            moved[0].wait_recv()
            level = candidate(index, rx.at[2 + index], moved[1:])
            store(tx.at[2 + index], level)
            if index < 2:
                moved = shift(3 + index, tx.at[2 + index], nxt, 1)
        for i in range(4):
            tx[5, i] = tx[4, i] - tx[3, i]
        chains = [shift(6 + j, tx.at[5], lax.rem(k + 1 + GROUP * j, n_tm), 2 * j + 1) for j in range(1, n_chain + 1)]
        moved = shift(5, tx.at[4], nxt, 1)
        carry = None
        for j in range(n_chain, 0, -1):
            for c in chains[j - 1]:
                c.wait_recv()
            gap = tuple(jnp.where(before >= GROUP * j, rx[6 + j, i], 0.0) for i in range(4))
            carry = gap if carry is None else tuple(a + b for a, b in zip(gap, carry))
            carry = lax.fori_loop(0, 2, lambda i, u: phi(u, speed[0] * speed[0], 8 * DT), carry)
        for c in moved:
            c.wait_recv()
        x_ref = rx.at[5]
        if carry is not None:
            for i in range(4):
                ys[4, i] = rx[5, i] + carry[i]
            x_ref = ys.at[4]
        level = candidate(3, x_ref, [])
        final = tx.at[7]
        for i in range(4):
            final[i] = tx[0, i] + level[i]
        moved = shift(6, final, nxt, 3)
        made = weights(4, slab_of(final))
        states_out[3] = final[:, mine]
        w = solve(4, made)
        rows = lax.broadcasted_iota(jnp.int32, w.shape, 0)
        lanes = lax.broadcasted_iota(jnp.int32, w.shape, 1)
        coords_out[...] = jnp.sum(jnp.where(rows == lanes, w, 0.0), axis=0, keepdims=True)[:, :rank]
        for c in moved:
            c.wait_recv()
        state = load(rx.at[6])
        for n in range(3):
            state = fine(n, state)
            store(acc4, state)
            states_out[n] = acc4[:, mine]
        for c in sent:
            c.wait_send()

    return kernel


def solution(mesh):
    n_tm, n_sp = mesh.shape["tm"], mesh.shape["space"]

    def body(speed, forcing, guess, basis):
        rank = basis.shape[1]
        slab, nx, ny = speed.shape
        nz = slab * n_sp
        n_chain = n_tm // GROUP - 1
        f32 = jnp.float32
        dma = pltpu.SemaphoreType.DMA
        return pl.pallas_call(
            make_kernel(n_tm, n_sp, rank, slab),
            out_shape=(
                jax.ShapeDtypeStruct((4, 4, slab, nx, ny), f32),
                jax.ShapeDtypeStruct((1, rank), f32),
            ),
            in_specs=[pl.BlockSpec(memory_space=pl.ANY)] * 4,
            out_specs=(pl.BlockSpec(memory_space=pltpu.VMEM),) * 2,
            scratch_shapes=[
                pltpu.VMEM((1, nz, nx, ny), f32),
                pltpu.VMEM((4, nz, nx, ny), f32),
                pltpu.VMEM((rank, 4 * slab, nx, ny), f32),
                pltpu.VMEM((7 + n_chain, 4, nz, nx, ny), f32),
                pltpu.VMEM((8, 4, nz, nx, ny), f32),
                pltpu.VMEM((5, 4, nz, nx, ny), f32),
                pltpu.VMEM((5, n_sp, 8, 2 * rank), f32),
                pltpu.VMEM((n_sp, rank, 2 * rank), f32),
                pltpu.VMEM((rank, 2 * rank), f32),
                pltpu.VMEM((2 * rank, ny), f32),
                pltpu.VMEM((rank, ny), f32),
                dma((4,)),
                dma((128 + 6 * n_sp,)), dma((128 + 6 * n_sp,)),
            ],
            compiler_params=pltpu.CompilerParams(
                collective_id=0, has_side_effects=True, vmem_limit_bytes=60 * 1024 * 1024
            ),
        )(speed[None], forcing, guess[0], basis[0].reshape(rank, 4 * slab, nx, ny))

    placed = (
        P("space", None, None),
        P("tm", "space", None, None),
        P("tm", None, "space", None, None),
        P("tm", None, None, "space", None, None),
    )
    return jax.shard_map(
        body,
        mesh=mesh,
        in_specs=placed,
        out_specs=(P("tm", None, "space", None, None), P("tm", None)),
        check_vma=False,
    )
```

profile of v0, /device:TPU:0, one launch (start us, length us, event | category | flops | bytes accessed | tf_op | source)
XLA Modules:
  0.0 82.3 jit_solution(5457037344042509245)
XLA Ops:
  0.6 78.9 %shard_map.59 = (f32[4,4,2,16,128]{4,3,2,1,0:T(8,128)}, f32[1,64]{1,0:T(1,128)}) custom-call(f32[1,2,16,128]{3,2,1,0:T(8,128)} %bitcast.5, f32[4,2,16,128]{3,2,1,0:T(8,128)} %forcing_in.1, f32[4,2,16,128]{3,2,1,0:T(8,128)} %bitcast.4, f32[64,8,16,128]{3,2,1,0:T(8,128)} %bitcast.3), custom_call_target="tpu_custom_call" | custom-call | tf_op jit(solution)/shard_map/pallas_call | solution.py:328
  79.5 1.7 %copy.8 = f32[4,4,2,16,128]{4,3,2,1,0:T(8,128)} copy(f32[4,4,2,16,128]{4,3,2,1,0:T(8,128)} %get-tuple-element.4) | data formatting | bytes 524288
  81.2 1.1 %copy.9 = f32[1,64]{1,0:T(1,128)} copy(f32[1,64]{1,0:T(1,128)} %get-tuple-element.5) | data formatting | bytes 512
where the time goes:
time: 82.5 us; the launch traced here: 82.3 us
  Pallas kernels  78.9 us (96%)
  local copies, waits for them, and re-layouts  2.8 us (3%)
    pallas_call x1, Pallas kernels, body(): pl.pallas_call(make_kernel(n_tm, n_sp, rank, slab), out_shape=(jax.ShapeD...  78.9 us
    unnamed x2, local copies, waits for them, and re-layouts  2.8 us

commit v1 on v0

v1 whole, which is shorter than its diff:
```python
import jax
import jax.numpy as jnp
from jax import lax
from jax.experimental import pallas as pl
from jax.experimental.pallas import tpu as pltpu
from jax.sharding import PartitionSpec as P

DT = 0.045
GROUP = 4
MESH = pl.DeviceIdType.MESH
VX, VY, VZ, DV, PR = range(5)


def make_kernel(n_tm, n_sp, rank, slab, nx, ny):
    n_chain = n_tm // GROUP - 1
    reach_max = max(4, 2 * n_chain)
    base = reach_max
    own_planes = range(base, base + slab)

    def span(lo, hi, first):
        lo, hi = max(lo, first), min(hi, first + slab)
        return (lo - first, hi - lo) if hi > lo else None

    def pieces(reach, keep):
        made = [] if keep is None else [(0, keep, 5 - keep, 0, slab)]
        far = -(-reach // slab)
        for dist in range(1, far + 1):
            for delta in (dist, -dist):
                first = base - delta * slab
                need = {
                    PR: span(base - reach, base + slab + reach, first),
                    DV: span(base - reach + 1, base + slab + reach - 1, first),
                }
                above = first + slab
                if base - reach + 1 <= above < base + slab + reach - 1:
                    need[VZ] = (slab - 1, 1)
                fields = sorted(need)
                at = 0
                while at < len(fields):
                    end = at + 1
                    while end < len(fields) and need[fields[end]] == need[fields[at]]:
                        end += 1
                    if need[fields[at]] is not None:
                        o, n = need[fields[at]]
                        made.append((delta, fields[at], end - at, o, n))
                    at = end
        return made

    def load_pieces(steps, keep):
        made = [(0, 0, steps, 0, slab)] if keep else []
        far = -(-(steps - 1) // slab)
        for dist in range(1, far + 1):
            for delta in (dist, -dist):
                first = base - delta * slab
                at = 0
                while at < steps - 1:
                    here = span(base - steps + 1 + at, base + slab + steps - 1 - at, first)
                    end = at + 1
                    while end < steps - 1 and here == span(
                        base - steps + 1 + end, base + slab + steps - 1 - end, first
                    ):
                        end += 1
                    if here is not None:
                        made.append((delta, at, end - at, here[0], here[1]))
                    at = end
        return made

    speed_pieces = [(d, 0, 1, o, n) for d, f, m, o, n in pieces(reach_max - 1, None) if f <= PR < f + m]

    def kernel(
        speed_in, forcing_in, guess_in, basis_in, states_out, coords_out,
        gl, fl, basis, cw, c2, fw, fo, wv, win, xs, tb, cf, gb, inv, acc, wb,
        local_sem, send_sems, recv_sems,
    ):
        k = lax.axis_index("tm")
        s = lax.axis_index("space")
        before = lax.rem(k + n_tm - 1, n_tm)

        def block(offset):
            return lax.rem(k + offset + n_tm, n_tm)

        def peer(d):
            return lax.rem(s + d, n_sp)

        def inside(at):
            return (at >= 0) & (at < n_sp)

        own = pl.ds(base, slab)
        copies = [
            pltpu.make_async_copy(guess_in, gl, local_sem.at[0]),
            pltpu.make_async_copy(forcing_in, fl, local_sem.at[1]),
            pltpu.make_async_copy(speed_in, cw.at[:, own], local_sem.at[2]),
            pltpu.make_async_copy(basis_in, basis, local_sem.at[3]),
        ]
        for c in copies:
            c.start()

        wins = {}
        senders = {}

        def name(key, reach):
            wins[key] = (win.at[len(wins)], reach)
            senders[key] = wv.at[len(senders)]

        name("guess", 4)
        name("relaxed", 4)
        for i in range(3):
            name(("x", i), 1)
            name(("y", i), 4)
        for j in range(1, n_chain + 1):
            name(("gap", j), 2 * j)
        name("x3", 1)
        name("y3", 4)
        name("final", 3)

        missing = {}
        for ref, reach in wins.values():
            for piece in pieces(reach, None):
                missing.setdefault(piece[0], []).append((ref, piece))
        for ref, part in ((fw, load_pieces(4, False)), (fo, load_pieces(3, False)), (cw, speed_pieces)):
            for piece in part:
                missing.setdefault(piece[0], []).append((ref, piece))
        for delta, regions in missing.items():
            def clear(regions=regions):
                for ref, (d, f, m, o, n) in regions:
                    at = base - d * slab + o
                    for i in range(f, f + m):
                        ref[i, at:at + n] = jnp.zeros((n, nx, ny), jnp.float32)

            pl.when(jnp.logical_not(inside(s - delta)))(clear)

        offsets = set()
        for off in [1, 2] + [GROUP * j for j in range(1, n_chain + 1)]:
            offsets |= {off % n_tm, -off % n_tm}
        partners = [(k, peer(d)) for d in range(1, n_sp)]
        for off in sorted(offsets - {0}):
            partners += [(block(off), peer(d)) for d in range(n_sp)]
        barrier = pltpu.get_barrier_semaphore()
        for target in partners:
            pl.semaphore_signal(barrier, inc=1, device_id=target, device_id_type=MESH)

        sent = []

        class Remote:
            def __init__(self, src, dst, target, sends=None, receives=None):
                i = len(sent)
                self.copy = pltpu.make_async_remote_copy(
                    src_ref=src, dst_ref=dst, send_sem=send_sems.at[i], recv_sem=recv_sems.at[i],
                    device_id=target, device_id_type=MESH,
                )
                self.sends, self.receives = sends, receives
                sent.append(self)
                self.under(sends, self.copy.start)

            def under(self, condition, act):
                if condition is None:
                    act()
                else:
                    pl.when(condition)(act)

            def wait_recv(self):
                self.under(self.receives, self.copy.wait_recv)

            def wait_send(self):
                self.under(self.sends, self.copy.wait_send)

        def both(a, b):
            return b if a is None else a if b is None else a & b

        def spread(src, at, dst, group, parts, sends=None, receives=None):
            made = []
            for delta, f, m, o, n in parts:
                made.append(Remote(
                    src.at[pl.ds(f, m), pl.ds(at + o, n)],
                    dst.at[pl.ds(f, m), pl.ds(base - delta * slab + o, n)],
                    (group, s + delta),
                    both(sends, None if delta == 0 else inside(s + delta)),
                    both(receives, None if delta == 0 else inside(s - delta)),
                ))
            return made

        def wait(made):
            for c in made:
                c.wait_recv()

        row = lax.broadcasted_iota(jnp.int32, (nx, ny), 0)
        lane = lax.broadcasted_iota(jnp.int32, (nx, ny), 1)
        first_row, last_row = row == 0, row == nx - 1
        first_lane, last_lane = lane == 0, lane == ny - 1

        def ahead(p, axis):
            n, last = ((nx, last_row), (ny, last_lane))[axis]
            return jnp.where(last, 0.0, pltpu.roll(p, n - 1, axis))

        def behind(p, axis, border):
            return jnp.where((first_row, first_lane)[axis], border, pltpu.roll(p, 1, axis))

        def floor(z):
            if z <= base and (base - z) % slab == 0:
                return jnp.where(s > (base - z) // slab, 1.0, 0.0)
            return None

        def lap(p, z):
            c = p[z]
            down = c - p[z - 1]
            edge = floor(z)
            if edge is not None:
                down = down * edge
            flat = (ahead(c, 0) + behind(c, 0, c)) + (ahead(c, 1) + behind(c, 1, c)) - 4.0 * c
            return flat + ((p[z + 1] - c) - down)

        def grad(p, z):
            c = p[z]
            return ahead(c, 0) - c, ahead(c, 1) - c, p[z + 1] - c

        def part_div(vx, vy, vz, z):
            d = (vx[z] - behind(vx[z], 0, 0.0)) + (vy[z] - behind(vy[z], 1, 0.0))
            return d + (vz[z] if z == base else vz[z] - vz[z - 1])

        def load_window(ref, reach):
            p = {z: ref[PR, z] for z in range(base - reach, base + slab + reach)}
            d = {}
            for z in range(base - reach + 1, base + slab + reach - 1):
                d[z] = ref[DV, z]
                if (z - base) % slab == 0:
                    d[z] = d[z] - ref[VZ, z - 1]
            return p, d

        def load_flow(ref):
            return tuple({z: ref[f, z] for z in own_planes} for f in (VX, VY, VZ))

        def store_state(ref, at, p, v):
            for z in own_planes:
                for f in (VX, VY, VZ):
                    ref[f, z - base + at] = v[f][z]
                ref[DV, z - base + at] = part_div(*v, z)
                ref[PR, z - base + at] = p[z]

        def scale(z, h):
            return h * c2[z]

        def evolve(p, d, steps, h, loads=None):
            total = None
            for i in range(steps):
                reach = steps - 1 - i
                kept = {z: p[z] for z in range(base, base + slab + 1)}
                total = kept if total is None else {z: total[z] + kept[z] for z in kept}
                fresh, nd = {}, {}
                for z in range(base - reach, base + slab + reach):
                    nd[z] = d[z] - h * lap(p, z)
                    fresh[z] = p[z] - scale(z, h) * nd[z]
                    if loads is not None:
                        fresh[z] = fresh[z] + loads(i, z)
                p, d = fresh, nd
            return p, d, total

        def push(v, total, h):
            out = ({}, {}, {})
            for z in own_planes:
                g = grad(total, z)
                for f in range(3):
                    out[f][z] = v[f][z] - h * g[f]
            return out

        def send(key, group, reach, keep, sends=None, receives=None):
            return spread(senders[key], 0, wins[key][0], group, pieces(reach, keep), sends, receives)

        copies[0].wait()
        p = {z: gl[0, z - base] for z in own_planes}
        v = tuple({z: gl[1 + f, z - base] for z in own_planes} for f in range(3))
        store_state(senders["guess"], 0, p, v)
        copies[1].wait()
        copies[2].wait()
        pl.semaphore_wait(barrier, len(partners))

        first = send("guess", block(2), 4, VX)
        first += spread(fl, 0, fw, block(1), load_pieces(4, True))
        first += spread(cw, base, cw, k, speed_pieces)

        copies[3].wait()

        def gram_step(i, total):
            t = jnp.swapaxes(basis[:, i], 0, 1)
            hi = t.astype(jnp.bfloat16)
            rest = t - hi.astype(jnp.float32)
            mid = rest.astype(jnp.bfloat16)
            low = (rest - mid.astype(jnp.float32)).astype(jnp.bfloat16)
            parts = jnp.concatenate([hi, mid, low], axis=1)
            flat = jnp.concatenate([parts[j] for j in range(parts.shape[0])], axis=1)
            return total + lax.dot_general(
                flat, flat, (((1,), (1,)), ((), ())), preferred_element_type=jnp.float32
            )

        full = lax.fori_loop(0, basis.shape[1], gram_step, jnp.zeros((3 * rank, 3 * rank), jnp.float32))
        hh, hm, hl = full[:rank, :rank], full[:rank, rank:2 * rank], full[:rank, 2 * rank:]
        mh, mm, lh = full[rank:2 * rank, :rank], full[rank:2 * rank, rank:2 * rank], full[2 * rank:, :rank]
        gram = hh + ((hm + mh) + (mm + (hl + lh)))
        gb[s] = jnp.concatenate([gram[:rank // 2], gram[rank // 2:]], axis=1)

        wait(first)
        for z in range(1, 2 * base + slab - 1):
            c2[z] = cw[0, z] * cw[0, z]

        def loads(i, z):
            return fw[i, z]

        p, d = load_window(wins["guess"][0], 4)
        p, d, total = evolve(p, d, 4, DT, loads)
        v = push(load_flow(wins["guess"][0]), total, DT)
        store_state(senders["relaxed"], 0, p, v)
        moved = send("relaxed", block(1), 4, VX)
        gram_copies = [Remote(gb.at[s], gb.at[s], (k, peer(d))) for d in range(1, n_sp)]
        late_loads = spread(fl, 0, fo, k, load_pieces(3, False))

        def dot(index, p, v):
            for z in own_planes:
                xs[z - base] = p[z]
                for f in range(3):
                    xs[(1 + f) * slab + z - base] = v[f][z]
            x = xs[...]

            def coef_step(i, carry):
                b = basis[pl.ds(8 * i, 8)]
                t = jnp.sum(b * x[None], axis=1)
                half = t.shape[1] // 2
                t = t[:, :half] + t[:, half:]
                acc[pl.ds(pl.multiple_of(8 * i, 8), 8), :] = jnp.sum(t, axis=1)
                return carry

            lax.fori_loop(0, rank // 8, coef_step, 0)
            ones = jnp.ones((8, acc.shape[1]), jnp.float32)
            cf[index, s] = lax.dot_general(
                ones, acc[...], (((1,), (1,)), ((), ())),
                precision=lax.Precision.HIGHEST, preferred_element_type=jnp.float32,
            )
            line = pl.ds(0, 1)
            return [
                Remote(cf.at[index, s, line], cf.at[index, s, line], (k, peer(d)))
                for d in range(1, n_sp)
            ]

        def solve(index, made):
            wait(made)
            total = cf[index, 0, 0:1]
            for i in range(1, n_sp):
                total = total + cf[index, i, 0:1]
            w = jnp.sum(inv[...] * total, axis=1, keepdims=True)
            return jnp.broadcast_to(w, wb.shape)

        def combine(index, made):
            wb[...] = solve(index, made)

            def sum_step(r, y):
                return y + wb[pl.ds(r, 1), :][None] * basis[r]

            y = lax.fori_loop(0, rank, sum_step, jnp.zeros(basis.shape[1:], jnp.float32), unroll=4)
            return [{z: y[f * slab + z - base] for z in own_planes} for f in range(4)]

        def store_y(ref, at, y):
            for z in own_planes:
                ref[VZ, z - base + at] = y[3][z]
                ref[DV, z - base + at] = part_div(*y[1:], z)
                ref[PR, z - base + at] = y[0][z]

        def coarse(ref):
            p, d = load_window(ref, 1)
            h = 4 * DT
            out = {z: p[z] - scale(z, h) * (d[z] - h * lap(p, z)) for z in own_planes}
            return out, push(load_flow(ref), {z: p[z] for z in range(base, base + slab + 1)}, h)

        def corrected(ref, p, v):
            q, d = load_window(ref, 4)
            h = 4 * DT
            late, _, total = evolve(q, d, 4, DT)
            change = {z: total[z] - 4.0 * q[z] for z in range(base, base + slab + 1)}
            out = {}
            for z in own_planes:
                out[z] = p[z] + (late[z] - (q[z] - scale(z, h) * (d[z] - h * lap(q, z))))
            return out, push(v, change, DT)

        wait(moved)
        p, d = load_window(wins["relaxed"][0], 4)
        p, d, total = evolve(p, d, 4, DT, loads)
        v = push(load_flow(wins["relaxed"][0]), total, DT)
        for z in own_planes:
            tb[0, 3, z - base] = p[z]
            for f in (VX, VY, VZ):
                tb[0, f, z - base] = v[f][z]
        rel = senders["relaxed"]
        p = {z: p[z] - rel[PR, z - base] for z in own_planes}
        v = tuple({z: v[f][z] - rel[f, z - base] for z in own_planes} for f in range(3))
        made = dot(0, p, v)
        store_state(senders[("x", 0)], 0, p, v)
        x_moved = send(("x", 0), block(1), 1, VX)

        wait(gram_copies)
        g = gb[0]
        for i in range(1, n_sp):
            g = g + gb[i]
        g = jnp.concatenate([g, pltpu.roll(g, rank, 1)], axis=0)
        rows = lax.broadcasted_iota(jnp.int32, g.shape, 0)
        lanes = lax.broadcasted_iota(jnp.int32, g.shape, 1)
        m = jnp.where(lanes < rank, g, jnp.where(lanes == rows + rank, 1.0, 0.0))
        for j in range(rank):
            pivot = m[j:j + 1]
            pivot = pivot / pivot[:, j:j + 1]
            m = jnp.where(rows == j, pivot, m - m[:, j:j + 1] * pivot)
        inverse = m[:, rank:]
        inv[...] = jnp.concatenate([inverse, jnp.zeros_like(inverse)], axis=1)

        res = senders[("x", 0)]
        back = []
        for i in range(3):
            y = combine(i, made)
            store_y(senders[("y", i)], 0, y)
            y_moved = send(("y", i), block(1), 4, VZ)
            if i == 0:

                back = [Remote(tb.at[0], tb.at[1], (before, s))]
            wait(x_moved)
            p, v = coarse(wins[("x", i)][0])
            p = {z: p[z] + res[PR, z - base] for z in own_planes}
            v = tuple({z: v[f][z] + res[f, z - base] for z in own_planes} for f in range(3))
            wait(y_moved)
            p, v = corrected(wins[("y", i)][0], p, v)
            if i < 2:
                made = dot(i + 1, p, v)
                store_state(senders[("x", i + 1)], 0, p, v)
                x_moved = send(("x", i + 1), block(1), 1, VX)

        old = senders[("x", 2)]
        gap_p = {z: p[z] - old[PR, z - base] for z in own_planes}
        gap_v = tuple({z: v[f][z] - old[f, z - base] for z in own_planes} for f in range(3))
        chains = []
        for j in range(1, n_chain + 1):
            if j == 1:
                store_state(senders[("gap", 1)], 0, gap_p, gap_v)
            chains.append(spread(
                senders[("gap", 1)], 0, wins[("gap", j)][0], block(GROUP * j), pieces(2 * j, VX),
                before + GROUP * j < n_tm, before >= GROUP * j,
            ))
        carry = None
        for j in range(n_chain, 0, -1):
            wait(chains[j - 1])
            ref = wins[("gap", j)][0]
            used = before >= GROUP * j
            q, d = load_window(ref, 2 * j)
            u = load_flow(ref)

            def kept(planes):
                return {z: jnp.where(used, planes[z], 0.0) for z in planes}

            q, d, u = kept(q), kept(d), tuple(kept(a) for a in u)
            if carry is not None:
                q = {z: q[z] + carry[0][z] for z in q}
                d = {z: d[z] + carry[1][z] for z in d}
                u = tuple({z: u[f][z] + carry[2][f][z] for z in own_planes} for f in range(3))
            for step in range(2):
                reach = 2 * j - 1 - step
                u = push(u, q, 8 * DT)
                nq, nd = {}, {}
                for z in range(base - reach, base + slab + reach):
                    nd[z] = d[z] - 8 * DT * lap(q, z)
                    nq[z] = q[z] - scale(z, 8 * DT) * nd[z]
                q, d = nq, nd
            carry = (q, d, u)
        if carry is not None:
            p = {z: p[z] + carry[0][z] for z in own_planes}
            v = tuple({z: v[f][z] + carry[2][f][z] for z in own_planes} for f in range(3))
        made = dot(3, p, v)
        ref = wins["x3"][0]
        store_state(ref, base, p, v)
        x_moved = spread(ref, base, ref, k, pieces(1, None))
        wait(x_moved)
        wait(back)
        p, v = coarse(ref)
        p = {z: p[z] + tb[1, 3, z - base] for z in own_planes}
        v = tuple({z: v[f][z] + tb[1, f, z - base] for z in own_planes} for f in range(3))
        y = combine(3, made)
        ref = wins["y3"][0]
        store_y(ref, base, y)
        y_moved = spread(ref, base, ref, k, pieces(4, None))
        wait(y_moved)
        p, v = corrected(ref, p, v)
        store_state(senders["final"], 0, p, v)
        moved = send("final", block(1), 3, VX)
        made = dot(4, p, v)
        for z in own_planes:
            states_out[3, 0, z - base] = p[z]
            for f in range(3):
                states_out[3, 1 + f, z - base] = v[f][z]
        w = solve(4, made)
        rows = lax.broadcasted_iota(jnp.int32, w.shape, 0)
        lanes = lax.broadcasted_iota(jnp.int32, w.shape, 1)
        coords_out[...] = jnp.sum(jnp.where(rows == lanes, w, 0.0), axis=0, keepdims=True)[:, :rank]
        wait(late_loads)
        wait(moved)
        p, d = load_window(wins["final"][0], 3)
        v = load_flow(wins["final"][0])
        for n in range(3):
            reach = 2 - n
            v = push(v, p, DT)
            fresh, nd = {}, {}
            for z in range(base - reach, base + slab + reach):
                nd[z] = d[z] - DT * lap(p, z)
                source = fl[n, z - base] if z in own_planes else fo[n, z]
                fresh[z] = (p[z] - scale(z, DT) * nd[z]) + source
            p, d = fresh, nd
            for z in own_planes:
                states_out[n, 0, z - base] = p[z]
                for f in range(3):
                    states_out[n, 1 + f, z - base] = v[f][z]
        for c in sent:
            c.wait_send()

    n_wins = 2 + 6 + n_chain + 3
    n_sent = (
        len(pieces(4, VX)) * 6 + len(pieces(3, VX)) * 2 + len(pieces(1, VX)) * 4
        + sum(len(pieces(2 * j, VX)) for j in range(1, n_chain + 1))
        + len(load_pieces(4, True)) + len(load_pieces(3, False)) + len(speed_pieces) + 6 * (n_sp - 1) + 1
    )
    return kernel, reach_max, n_wins, n_sent


def solution(mesh):
    n_tm, n_sp = mesh.shape["tm"], mesh.shape["space"]

    def body(speed, forcing, guess, basis):
        rank = basis.shape[1]
        slab, nx, ny = speed.shape
        f32 = jnp.float32
        dma = pltpu.SemaphoreType.DMA
        kernel, reach, n_wins, n_sent = make_kernel(n_tm, n_sp, rank, slab, nx, ny)
        wide = slab + 2 * reach
        return pl.pallas_call(
            kernel,
            out_shape=(
                jax.ShapeDtypeStruct((4, 4, slab, nx, ny), f32),
                jax.ShapeDtypeStruct((1, rank), f32),
            ),
            in_specs=[pl.BlockSpec(memory_space=pl.ANY)] * 4,
            out_specs=(pl.BlockSpec(memory_space=pltpu.VMEM),) * 2,
            scratch_shapes=[
                pltpu.VMEM((4, slab, nx, ny), f32),
                pltpu.VMEM((4, slab, nx, ny), f32),
                pltpu.VMEM((rank, 4 * slab, nx, ny), f32),
                pltpu.VMEM((1, wide, nx, ny), f32),
                pltpu.VMEM((wide, nx, ny), f32),
                pltpu.VMEM((4, wide, nx, ny), f32),
                pltpu.VMEM((3, wide, nx, ny), f32),
                pltpu.VMEM((n_wins, 5, slab, nx, ny), f32),
                pltpu.VMEM((n_wins, 5, wide, nx, ny), f32),
                pltpu.VMEM((4 * slab, nx, ny), f32),
                pltpu.VMEM((2, 4, slab, nx, ny), f32),
                pltpu.VMEM((5, n_sp, 8, 2 * rank), f32),
                pltpu.VMEM((n_sp, rank // 2, 2 * rank), f32),
                pltpu.VMEM((rank, 2 * rank), f32),
                pltpu.VMEM((2 * rank, ny), f32),
                pltpu.VMEM((rank, ny), f32),
                dma((4,)),
                dma((n_sent,)), dma((n_sent,)),
            ],
            compiler_params=pltpu.CompilerParams(
                collective_id=0, has_side_effects=True, vmem_limit_bytes=60 * 1024 * 1024
            ),
        )(speed[None], forcing, guess[0], basis[0].reshape(rank, 4 * slab, nx, ny))

    placed = (
        P("space", None, None),
        P("tm", "space", None, None),
        P("tm", None, "space", None, None),
        P("tm", None, None, "space", None, None),
    )
    return jax.shard_map(
        body,
        mesh=mesh,
        in_specs=placed,
        out_specs=(P("tm", None, "space", None, None), P("tm", None)),
        check_vma=False,
    )
```

time: 82.5 us -> 70.1 us (0.85)
  Pallas kernels: 78.9 us -> 66.5 us
    pallas_call x1, Pallas kernels: 78.9 us -> 66.5 us  [body(): pl.pallas_call(kernel, out_shape=(jax.ShapeDtypeStruct((4, 4, slab, nx, n...]
where the time goes in v1:
time: 70.1 us; the launch traced here: 70 us
  Pallas kernels  66.5 us (95%)
  local copies, waits for them, and re-layouts  2.8 us (4%)
    pallas_call x1, Pallas kernels, body(): pl.pallas_call(kernel, out_shape=(jax.ShapeDtypeStruct((4, 4, slab, nx, n...  66.5 us
    unnamed x2, local copies, waits for them, and re-layouts  2.8 us

profile of v1, /device:TPU:0, one launch (start us, length us, event | category | flops | bytes accessed | tf_op | source)
XLA Modules:
  0.0 70.0 jit_solution(17580114940078035784)
XLA Ops:
  0.6 66.5 %shard_map.59 = (f32[4,4,2,16,128]{4,3,2,1,0:T(8,128)}, f32[1,64]{1,0:T(1,128)}) custom-call(f32[1,2,16,128]{3,2,1,0:T(8,128)} %bitcast.5, f32[4,2,16,128]{3,2,1,0:T(8,128)} %forcing_in.1, f32[4,2,16,128]{3,2,1,0:T(8,128)} %bitcast.4, f32[64,8,16,128]{3,2,1,0:T(8,128)} %bitcast.3), custom_call_target="tpu_custom_call" | custom-call | tf_op jit(solution)/shard_map/pallas_call | solution.py:535
  67.2 1.7 %copy.8 = f32[4,4,2,16,128]{4,3,2,1,0:T(8,128)} copy(f32[4,4,2,16,128]{4,3,2,1,0:T(8,128)} %get-tuple-element.4) | data formatting | bytes 524288
  68.8 1.1 %copy.9 = f32[1,64]{1,0:T(1,128)} copy(f32[1,64]{1,0:T(1,128)} %get-tuple-element.5) | data formatting | bytes 512

commit v2 on v1

--- a/solution.py
+++ b/solution.py
@@ -21,10 +21,10 @@
         lo, hi = max(lo, first), min(hi, first + slab)
         return (lo - first, hi - lo) if hi > lo else None
 
-    def pieces(reach, keep):
-        made = [] if keep is None else [(0, keep, 5 - keep, 0, slab)]
+    def pieces(reach, here, patch):
+        made = []
         far = -(-reach // slab)
-        for dist in range(1, far + 1):
+        for dist in range(far, 0, -1):
             for delta in (dist, -dist):
                 first = base - delta * slab
                 need = {
@@ -32,7 +32,7 @@
                     DV: span(base - reach + 1, base + slab + reach - 1, first),
                 }
                 above = first + slab
-                if base - reach + 1 <= above < base + slab + reach - 1:
+                if patch and base - reach + 1 <= above < base + slab + reach - 1:
                     need[VZ] = (slab - 1, 1)
                 fields = sorted(need)
                 at = 0
@@ -44,12 +44,19 @@
                         o, n = need[fields[at]]
                         made.append((delta, fields[at], end - at, o, n))
                     at = end
+        if here:
+            made.append((0, DV, 2, 0, slab))
+            if patch and reach > 1:
+                made.append((0, VZ, 1, slab - 1, 1))
         return made
 
+    flow = [(0, VX, 3, 0, slab)]
+    rest = [(0, VX, 2, 0, slab)] + ([(0, VZ, 1, 0, slab - 1)] if slab > 1 else [])
+
     def load_pieces(steps, keep):
-        made = [(0, 0, steps, 0, slab)] if keep else []
+        made = []
         far = -(-(steps - 1) // slab)
-        for dist in range(1, far + 1):
+        for dist in range(far, 0, -1):
             for delta in (dist, -dist):
                 first = base - delta * slab
                 at = 0
@@ -63,13 +70,15 @@
                     if here is not None:
                         made.append((delta, at, end - at, here[0], here[1]))
                     at = end
+        if keep:
+            made.append((0, 0, steps, 0, slab))
         return made
 
-    speed_pieces = [(d, 0, 1, o, n) for d, f, m, o, n in pieces(reach_max - 1, None) if f <= PR < f + m]
+    speed_pieces = [(d, 0, 1, o, n) for d, f, m, o, n in pieces(reach_max - 1, False, False) if f <= PR < f + m]
 
     def kernel(
         speed_in, forcing_in, guess_in, basis_in, states_out, coords_out,
-        gl, fl, basis, cw, c2, fw, fo, wv, win, xs, tb, cf, gb, inv, acc, wb,
+        gl, fl, basis, slim, cw, c2, fw, fo, wv, win, xs, tb, cf, gb, inv, acc, wb,
         local_sem, send_sems, recv_sems,
     ):
         k = lax.axis_index("tm")
@@ -77,13 +86,44 @@
         before = lax.rem(k + n_tm - 1, n_tm)
 
         def block(offset):
-            return lax.rem(k + offset + n_tm, n_tm)
+            return lax.rem(k + offset % n_tm, n_tm)
 
         def peer(d):
             return lax.rem(s + d, n_sp)
 
         def inside(at):
             return (at >= 0) & (at < n_sp)
+
+
+        barrier = pltpu.get_barrier_semaphore()
+
+        def greet(group, at, condition):
+            def act():
+                pl.semaphore_signal(barrier, inc=1, device_id=(group, at), device_id_type=MESH)
+
+            if condition is None:
+                act()
+            else:
+                pl.when(condition)(act)
+
+        def deltas(reach):
+            return sorted({piece[0] for piece in pieces(reach, True, False)}, key=abs)[::-1]
+
+        def one(condition):
+            return jnp.where(condition, 1, 0)
+
+        greetings = n_sp
+        for off, reach in [(1, 4), (2, 4)]:
+            for delta in deltas(reach):
+                greet(block(-off), s - delta, None if delta == 0 else inside(s - delta))
+                greetings += 1 if delta == 0 else one(inside(s + delta))
+        for d in range(n_sp - 1, 0, -1):
+            greet(k, peer(d), None)
+        for j in range(1, n_chain + 1):
+            for delta in deltas(2 * j):
+                greet(block(-GROUP * j), s - delta, (before >= GROUP * j) & inside(s - delta))
+                greetings += one((before + GROUP * j < n_tm) & inside(s + delta))
+        greet(block(1), s, None)
 
         own = pl.ds(base, slab)
         copies = [
@@ -102,20 +142,21 @@
             wins[key] = (win.at[len(wins)], reach)
             senders[key] = wv.at[len(senders)]
 
-        name("guess", 4)
-        name("relaxed", 4)
+        patched = ("guess", "y")
+        name(("guess", 0), 4)
+        name(("relaxed", 0), 4)
         for i in range(3):
             name(("x", i), 1)
             name(("y", i), 4)
         for j in range(1, n_chain + 1):
             name(("gap", j), 2 * j)
-        name("x3", 1)
-        name("y3", 4)
-        name("final", 3)
+        name(("x", 3), 1)
+        name(("y", 3), 4)
+        name(("final", 0), 3)
 
         missing = {}
-        for ref, reach in wins.values():
-            for piece in pieces(reach, None):
+        for key, (ref, reach) in wins.items():
+            for piece in pieces(reach, False, key[0] in patched):
                 missing.setdefault(piece[0], []).append((ref, piece))
         for ref, part in ((fw, load_pieces(4, False)), (fo, load_pieces(3, False)), (cw, speed_pieces)):
             for piece in part:
@@ -128,16 +169,6 @@
                         ref[i, at:at + n] = jnp.zeros((n, nx, ny), jnp.float32)
 
             pl.when(jnp.logical_not(inside(s - delta)))(clear)
-
-        offsets = set()
-        for off in [1, 2] + [GROUP * j for j in range(1, n_chain + 1)]:
-            offsets |= {off % n_tm, -off % n_tm}
-        partners = [(k, peer(d)) for d in range(1, n_sp)]
-        for off in sorted(offsets - {0}):
-            partners += [(block(off), peer(d)) for d in range(n_sp)]
-        barrier = pltpu.get_barrier_semaphore()
-        for target in partners:
-            pl.semaphore_signal(barrier, inc=1, device_id=target, device_id_type=MESH)
 
         sent = []
 
@@ -217,24 +248,40 @@
             d = (vx[z] - behind(vx[z], 0, 0.0)) + (vy[z] - behind(vy[z], 1, 0.0))
             return d + (vz[z] if z == base else vz[z] - vz[z - 1])
 
-        def load_window(ref, reach):
+        def load_window(ref, reach, patch=False):
             p = {z: ref[PR, z] for z in range(base - reach, base + slab + reach)}
             d = {}
             for z in range(base - reach + 1, base + slab + reach - 1):
                 d[z] = ref[DV, z]
-                if (z - base) % slab == 0:
+                if patch and (z - base) % slab == 0:
                     d[z] = d[z] - ref[VZ, z - 1]
             return p, d
 
         def load_flow(ref):
             return tuple({z: ref[f, z] for z in own_planes} for f in (VX, VY, VZ))
 
-        def store_state(ref, at, p, v):
+        def store_wave(ref, p, d):
+            for z in own_planes:
+                ref[DV, z - base] = d[z]
+                ref[PR, z - base] = p[z]
+
+        def store_flow(ref, v):
             for z in own_planes:
                 for f in (VX, VY, VZ):
-                    ref[f, z - base + at] = v[f][z]
-                ref[DV, z - base + at] = part_div(*v, z)
-                ref[PR, z - base + at] = p[z]
+                    ref[f, z - base] = v[f][z]
+
+        def load_state(ref):
+            p, d = ({z: ref[f, z - base] for z in own_planes} for f in (PR, DV))
+            return p, tuple({z: ref[f, z - base] for z in own_planes} for f in (VX, VY, VZ)), d
+
+        def plus(a, b):
+            return {z: a[z] + b[z] for z in own_planes}
+
+        def minus(a, b):
+            return {z: a[z] - b[z] for z in own_planes}
+
+        def each(op, a, b):
+            return op(a[0], b[0]), tuple(op(x, y) for x, y in zip(a[1], b[1])), op(a[2], b[2])
 
         def scale(z, h):
             return h * c2[z]
@@ -262,21 +309,17 @@
                     out[f][z] = v[f][z] - h * g[f]
             return out
 
-        def send(key, group, reach, keep, sends=None, receives=None):
-            return spread(senders[key], 0, wins[key][0], group, pieces(reach, keep), sends, receives)
+        def send(key, group, reach):
+            return spread(senders[key], 0, wins[key][0], group, pieces(reach, True, key[0] in patched))
+
+        def send_flow(key, group):
+            return spread(senders[key], 0, wins[key][0], group, rest if key[0] in patched else flow)
 
         copies[0].wait()
         p = {z: gl[0, z - base] for z in own_planes}
         v = tuple({z: gl[1 + f, z - base] for z in own_planes} for f in range(3))
-        store_state(senders["guess"], 0, p, v)
-        copies[1].wait()
-        copies[2].wait()
-        pl.semaphore_wait(barrier, len(partners))
-
-        first = send("guess", block(2), 4, VX)
-        first += spread(fl, 0, fw, block(1), load_pieces(4, True))
-        first += spread(cw, base, cw, k, speed_pieces)
-
+        store_wave(senders[("guess", 0)], p, {z: part_div(*v, z) for z in own_planes})
+        store_flow(senders[("guess", 0)], v)
         copies[3].wait()
 
         def gram_step(i, total):
@@ -291,12 +334,35 @@
                 flat, flat, (((1,), (1,)), ((), ())), preferred_element_type=jnp.float32
             )
 
-        full = lax.fori_loop(0, basis.shape[1], gram_step, jnp.zeros((3 * rank, 3 * rank), jnp.float32))
+        early = 0
+        full = lax.fori_loop(0, early, gram_step, jnp.zeros((3 * rank, 3 * rank), jnp.float32))
+        copies[1].wait()
+        copies[2].wait()
+        pl.semaphore_wait(barrier, greetings)
+
+        first = send(("guess", 0), block(2), 4)
+        first += spread(fl, 0, fw, block(1), load_pieces(4, True))
+        first += spread(cw, base, cw, k, speed_pieces)
+        first_flow = send_flow(("guess", 0), block(2))
+
+        full = lax.fori_loop(early, basis.shape[1], gram_step, full)
         hh, hm, hl = full[:rank, :rank], full[:rank, rank:2 * rank], full[:rank, 2 * rank:]
         mh, mm, lh = full[rank:2 * rank, :rank], full[rank:2 * rank, rank:2 * rank], full[2 * rank:, :rank]
         gram = hh + ((hm + mh) + (mm + (hl + lh)))
         gb[s] = jnp.concatenate([gram[:rank // 2], gram[rank // 2:]], axis=1)
 
+        gram_copies = [Remote(gb.at[s], gb.at[s], (k, peer(d))) for d in range(1, n_sp)]
+
+        def narrow_step(r, carry):
+            b = [{z: basis[r, f * slab + z - base] for z in own_planes} for f in range(4)]
+            for z in own_planes:
+                slim[r, z - base] = part_div(*b[1:], z)
+                slim[r, slab + z - base] = b[0][z]
+            slim[r, 2 * slab] = b[3][base + slab - 1]
+            return carry
+
+        lax.fori_loop(0, rank, narrow_step, 0, unroll=2)
+
         wait(first)
         for z in range(1, 2 * base + slab - 1):
             c2[z] = cw[0, z] * cw[0, z]
@@ -304,13 +370,14 @@
         def loads(i, z):
             return fw[i, z]
 
-        p, d = load_window(wins["guess"][0], 4)
+        p, d = load_window(wins[("guess", 0)][0], 4, True)
         p, d, total = evolve(p, d, 4, DT, loads)
-        v = push(load_flow(wins["guess"][0]), total, DT)
-        store_state(senders["relaxed"], 0, p, v)
-        moved = send("relaxed", block(1), 4, VX)
-        gram_copies = [Remote(gb.at[s], gb.at[s], (k, peer(d))) for d in range(1, n_sp)]
-        late_loads = spread(fl, 0, fo, k, load_pieces(3, False))
+        rel = senders[("relaxed", 0)]
+        store_wave(rel, p, d)
+        moved = send(("relaxed", 0), block(1), 4)
+        wait(first_flow)
+        store_flow(rel, push(load_flow(wins[("guess", 0)][0]), total, DT))
+        moved_flow = send_flow(("relaxed", 0), block(1))
 
         def dot(index, p, v):
             for z in own_planes:
@@ -347,51 +414,35 @@
             w = jnp.sum(inv[...] * total, axis=1, keepdims=True)
             return jnp.broadcast_to(w, wb.shape)
 
-        def combine(index, made):
+        def combine(index, made, ref, at):
             wb[...] = solve(index, made)
 
             def sum_step(r, y):
-                return y + wb[pl.ds(r, 1), :][None] * basis[r]
-
-            y = lax.fori_loop(0, rank, sum_step, jnp.zeros(basis.shape[1:], jnp.float32), unroll=4)
-            return [{z: y[f * slab + z - base] for z in own_planes} for f in range(4)]
-
-        def store_y(ref, at, y):
+                return y + wb[pl.ds(r, 1), :][None] * slim[r]
+
+            y = lax.fori_loop(0, rank, sum_step, jnp.zeros(slim.shape[1:], jnp.float32), unroll=8)
+            for i in range(slab):
+                ref[DV, at + i] = y[i]
+                ref[PR, at + i] = y[slab + i]
+            ref[VZ, at + slab - 1] = y[2 * slab]
+
+        def coarse(p, d, v):
+            h = 4 * DT
+            nd = {z: d[z] - h * lap(p, z) for z in own_planes}
+            out = {z: p[z] - scale(z, h) * nd[z] for z in own_planes}
+            return out, push(v, {z: p[z] for z in range(base, base + slab + 1)}, h), nd
+
+        def corrected(ref, p, v, d):
+            q, e = load_window(ref, 4, True)
+            h = 4 * DT
+            late, ne, total = evolve(q, e, 4, DT)
+            change = {z: total[z] - 4.0 * q[z] for z in range(base, base + slab + 1)}
+            out, od = {}, {}
             for z in own_planes:
-                ref[VZ, z - base + at] = y[3][z]
-                ref[DV, z - base + at] = part_div(*y[1:], z)
-                ref[PR, z - base + at] = y[0][z]
-
-        def coarse(ref):
-            p, d = load_window(ref, 1)
-            h = 4 * DT
-            out = {z: p[z] - scale(z, h) * (d[z] - h * lap(p, z)) for z in own_planes}
-            return out, push(load_flow(ref), {z: p[z] for z in range(base, base + slab + 1)}, h)
-
-        def corrected(ref, p, v):
-            q, d = load_window(ref, 4)
-            h = 4 * DT
-            late, _, total = evolve(q, d, 4, DT)
-            change = {z: total[z] - 4.0 * q[z] for z in range(base, base + slab + 1)}
-            out = {}
-            for z in own_planes:
-                out[z] = p[z] + (late[z] - (q[z] - scale(z, h) * (d[z] - h * lap(q, z))))
-            return out, push(v, change, DT)
-
-        wait(moved)
-        p, d = load_window(wins["relaxed"][0], 4)
-        p, d, total = evolve(p, d, 4, DT, loads)
-        v = push(load_flow(wins["relaxed"][0]), total, DT)
-        for z in own_planes:
-            tb[0, 3, z - base] = p[z]
-            for f in (VX, VY, VZ):
-                tb[0, f, z - base] = v[f][z]
-        rel = senders["relaxed"]
-        p = {z: p[z] - rel[PR, z - base] for z in own_planes}
-        v = tuple({z: v[f][z] - rel[f, z - base] for z in own_planes} for f in range(3))
-        made = dot(0, p, v)
-        store_state(senders[("x", 0)], 0, p, v)
-        x_moved = send(("x", 0), block(1), 1, VX)
+                ce = e[z] - h * lap(q, z)
+                out[z] = p[z] + (late[z] - (q[z] - scale(z, h) * ce))
+                od[z] = d[z] + (ne[z] - ce)
+            return out, push(v, change, DT), od
 
         wait(gram_copies)
         g = gb[0]
@@ -401,42 +452,78 @@
         rows = lax.broadcasted_iota(jnp.int32, g.shape, 0)
         lanes = lax.broadcasted_iota(jnp.int32, g.shape, 1)
         m = jnp.where(lanes < rank, g, jnp.where(lanes == rows + rank, 1.0, 0.0))
-        for j in range(rank):
-            pivot = m[j:j + 1]
-            pivot = pivot / pivot[:, j:j + 1]
-            m = jnp.where(rows == j, pivot, m - m[:, j:j + 1] * pivot)
+        def eliminate(m, first, last):
+            for j in range(first, last, width):
+                part = [jnp.broadcast_to(m[j + i:j + i + 1], (8, m.shape[1])) for i in range(width)]
+                e = [[jnp.broadcast_to(r[:, j + i:j + i + 1], r.shape) for i in range(width)] for r in part]
+                columns = [m[:, j + i:j + i + 1] for i in range(width)]
+                for t in range(width):
+                    scaled = 1.0 / e[t][t]
+                    part[t] = part[t] * scaled
+                    e[t] = [x * scaled for x in e[t]]
+                    for i in range(width):
+                        if i != t:
+                            f = e[i][t]
+                            part[i] = part[i] - f * part[t]
+                            e[i] = [x - f * y for x, y in zip(e[i], e[t])]
+                for i in range(width):
+                    m = m - jnp.where((rows >= j) & (rows < j + width), 0.0, columns[i]) * part[i][:1]
+                for i in range(width):
+                    m = jnp.where(rows == j + i, part[i][:1], m)
+            return m
+
+        width = 4 if rank % 4 == 0 else 1
+        half = rank // 2 // width * width
+        m = eliminate(m, 0, half)
+        wait(moved)
+        wait(moved_flow)
+        p, d = load_window(wins[("relaxed", 0)][0], 4)
+        p, d, total = evolve(p, d, 4, DT, loads)
+        v = push(load_flow(wins[("relaxed", 0)][0]), total, DT)
+        store_wave(tb.at[0], p, d)
+        store_flow(tb.at[0], v)
+        x = each(minus, (p, v, d), load_state(rel))
+
+        def send_level(i):
+            ref = senders[("x", i)]
+            store_wave(ref, x[0], x[2])
+            store_flow(ref, x[1])
+            return send(("x", i), block(1), 1) + send_flow(("x", i), block(1))
+
+        made = dot(0, x[0], x[1])
+        x_moved = send_level(0)
+        m = eliminate(m, half, rank)
         inverse = m[:, rank:]
         inv[...] = jnp.concatenate([inverse, jnp.zeros_like(inverse)], axis=1)
 
         res = senders[("x", 0)]
         back = []
         for i in range(3):
-            y = combine(i, made)
-            store_y(senders[("y", i)], 0, y)
-            y_moved = send(("y", i), block(1), 4, VZ)
+            combine(i, made, senders[("y", i)], 0)
+            y_moved = send(("y", i), block(1), 4)
             if i == 0:
-
                 back = [Remote(tb.at[0], tb.at[1], (before, s))]
+            if i == 1:
+                late_loads = spread(fl, 0, fo, k, load_pieces(3, False))
             wait(x_moved)
-            p, v = coarse(wins[("x", i)][0])
-            p = {z: p[z] + res[PR, z - base] for z in own_planes}
-            v = tuple({z: v[f][z] + res[f, z - base] for z in own_planes} for f in range(3))
+            ref = wins[("x", i)][0]
+            p, d = load_window(ref, 1)
+            x = each(plus, coarse(p, d, load_flow(ref)), load_state(res))
             wait(y_moved)
-            p, v = corrected(wins[("y", i)][0], p, v)
+            x = corrected(wins[("y", i)][0], *x)
             if i < 2:
-                made = dot(i + 1, p, v)
-                store_state(senders[("x", i + 1)], 0, p, v)
-                x_moved = send(("x", i + 1), block(1), 1, VX)
-
-        old = senders[("x", 2)]
-        gap_p = {z: p[z] - old[PR, z - base] for z in own_planes}
-        gap_v = tuple({z: v[f][z] - old[f, z - base] for z in own_planes} for f in range(3))
+                made = dot(i + 1, x[0], x[1])
+                x_moved = send_level(i + 1)
+
         chains = []
+        if n_chain:
+            gap = each(minus, x, load_state(senders[("x", 2)]))
+            ref = senders[("gap", 1)]
+            store_wave(ref, gap[0], gap[2])
+            store_flow(ref, gap[1])
         for j in range(1, n_chain + 1):
-            if j == 1:
-                store_state(senders[("gap", 1)], 0, gap_p, gap_v)
             chains.append(spread(
-                senders[("gap", 1)], 0, wins[("gap", j)][0], block(GROUP * j), pieces(2 * j, VX),
+                senders[("gap", 1)], 0, wins[("gap", j)][0], block(GROUP * j), pieces(2 * j, True, False) + flow,
                 before + GROUP * j < n_tm, before >= GROUP * j,
             ))
         carry = None
@@ -465,25 +552,24 @@
                 q, d = nq, nd
             carry = (q, d, u)
         if carry is not None:
-            p = {z: p[z] + carry[0][z] for z in own_planes}
-            v = tuple({z: v[f][z] + carry[2][f][z] for z in own_planes} for f in range(3))
-        made = dot(3, p, v)
-        ref = wins["x3"][0]
-        store_state(ref, base, p, v)
-        x_moved = spread(ref, base, ref, k, pieces(1, None))
+            x = each(plus, x, (carry[0], carry[2], carry[1]))
+        made = dot(3, x[0], x[1])
+        ref = wins[("x", 3)][0]
+        for z in own_planes:
+            ref[PR, z] = x[0][z]
+        x_moved = spread(ref, base, ref, k, pieces(1, False, False))
         wait(x_moved)
         wait(back)
-        p, v = coarse(ref)
-        p = {z: p[z] + tb[1, 3, z - base] for z in own_planes}
-        v = tuple({z: v[f][z] + tb[1, f, z - base] for z in own_planes} for f in range(3))
-        y = combine(3, made)
-        ref = wins["y3"][0]
-        store_y(ref, base, y)
-        y_moved = spread(ref, base, ref, k, pieces(4, None))
+        x = each(plus, coarse(load_window(ref, 1)[0], x[2], x[1]), load_state(tb.at[1]))
+        ref = wins[("y", 3)][0]
+        combine(3, made, ref, base)
+        y_moved = spread(ref, base, ref, k, pieces(4, False, True))
         wait(y_moved)
-        p, v = corrected(ref, p, v)
-        store_state(senders["final"], 0, p, v)
-        moved = send("final", block(1), 3, VX)
+        p, v, d = corrected(ref, *x)
+        ref = senders[("final", 0)]
+        store_wave(ref, p, d)
+        store_flow(ref, v)
+        moved = send(("final", 0), block(1), 3) + send_flow(("final", 0), block(1))
         made = dot(4, p, v)
         for z in own_planes:
             states_out[3, 0, z - base] = p[z]
@@ -495,8 +581,8 @@
         coords_out[...] = jnp.sum(jnp.where(rows == lanes, w, 0.0), axis=0, keepdims=True)[:, :rank]
         wait(late_loads)
         wait(moved)
-        p, d = load_window(wins["final"][0], 3)
-        v = load_flow(wins["final"][0])
+        p, d = load_window(wins[("final", 0)][0], 3)
+        v = load_flow(wins[("final", 0)][0])
         for n in range(3):
             reach = 2 - n
             v = push(v, p, DT)
@@ -515,8 +601,8 @@
 
     n_wins = 2 + 6 + n_chain + 3
     n_sent = (
-        len(pieces(4, VX)) * 6 + len(pieces(3, VX)) * 2 + len(pieces(1, VX)) * 4
-        + sum(len(pieces(2 * j, VX)) for j in range(1, n_chain + 1))
+        len(pieces(4, True, True)) * 6 + len(pieces(3, True, False)) + len(pieces(1, True, False)) * 4
+        + sum(len(pieces(2 * j, True, False)) + 1 for j in range(1, n_chain + 1)) + 7
         + len(load_pieces(4, True)) + len(load_pieces(3, False)) + len(speed_pieces) + 6 * (n_sp - 1) + 1
     )
     return kernel, reach_max, n_wins, n_sent
@@ -538,12 +624,13 @@
                 jax.ShapeDtypeStruct((4, 4, slab, nx, ny), f32),
                 jax.ShapeDtypeStruct((1, rank), f32),
             ),
-            in_specs=[pl.BlockSpec(memory_space=pl.ANY)] * 4,
+            in_specs=[pl.BlockSpec(memory_space=pltpu.HBM)] * 4,
             out_specs=(pl.BlockSpec(memory_space=pltpu.VMEM),) * 2,
             scratch_shapes=[
                 pltpu.VMEM((4, slab, nx, ny), f32),
                 pltpu.VMEM((4, slab, nx, ny), f32),
                 pltpu.VMEM((rank, 4 * slab, nx, ny), f32),
+                pltpu.VMEM((rank, 2 * slab + 1, nx, ny), f32),
                 pltpu.VMEM((1, wide, nx, ny), f32),
                 pltpu.VMEM((wide, nx, ny), f32),
                 pltpu.VMEM((4, wide, nx, ny), f32),
@@ -551,7 +638,7 @@
                 pltpu.VMEM((n_wins, 5, slab, nx, ny), f32),
                 pltpu.VMEM((n_wins, 5, wide, nx, ny), f32),
                 pltpu.VMEM((4 * slab, nx, ny), f32),
-                pltpu.VMEM((2, 4, slab, nx, ny), f32),
+                pltpu.VMEM((2, 5, slab, nx, ny), f32),
                 pltpu.VMEM((5, n_sp, 8, 2 * rank), f32),
                 pltpu.VMEM((n_sp, rank // 2, 2 * rank), f32),
                 pltpu.VMEM((rank, 2 * rank), f32),

time: 70.1 us -> 64.1 us (0.914)
  Pallas kernels: 66.5 us -> 60.4 us
    pallas_call x1, Pallas kernels: 66.5 us -> 60.4 us  [body(): pl.pallas_call(kernel, out_shape=(jax.ShapeDtypeStruct((4, 4, slab, nx, n...]
where the time goes in v2:
time: 64.1 us; the launch traced here: 63.9 us
  Pallas kernels  60.4 us (94%)
  local copies, waits for them, and re-layouts  2.8 us (4%)
    pallas_call x1, Pallas kernels, body(): pl.pallas_call(kernel, out_shape=(jax.ShapeDtypeStruct((4, 4, slab, nx, n...  60.4 us
    unnamed x2, local copies, waits for them, and re-layouts  2.8 us

profile of v2, /device:TPU:0, one launch (start us, length us, event | category | flops | bytes accessed | tf_op | source)
XLA Modules:
  0.0 63.9 jit_solution(2900399726403188377)
XLA Ops:
  0.6 60.4 %shard_map.59 = (f32[4,4,2,16,128]{4,3,2,1,0:T(8,128)}, f32[1,64]{1,0:T(1,128)}) custom-call(f32[1,2,16,128]{3,2,1,0:T(8,128)} %bitcast.5, f32[4,2,16,128]{3,2,1,0:T(8,128)} %forcing_in.1, f32[4,2,16,128]{3,2,1,0:T(8,128)} %bitcast.4, f32[64,8,16,128]{3,2,1,0:T(8,128)} %bitcast.3), custom_call_target="tpu_custom_call" | custom-call | tf_op jit(solution)/shard_map/pallas_call | solution.py:621
  61.1 1.7 %copy.8 = f32[4,4,2,16,128]{4,3,2,1,0:T(8,128)} copy(f32[4,4,2,16,128]{4,3,2,1,0:T(8,128)} %get-tuple-element.4) | data formatting | bytes 524288
  62.7 1.1 %copy.9 = f32[1,64]{1,0:T(1,128)} copy(f32[1,64]{1,0:T(1,128)} %get-tuple-element.5) | data formatting | bytes 512

commit v3 on v2

--- a/solution.py
+++ b/solution.py
@@ -315,6 +315,7 @@
         def send_flow(key, group):
             return spread(senders[key], 0, wins[key][0], group, rest if key[0] in patched else flow)
 
+        acc[rank:, :] = jnp.zeros((acc.shape[0] - rank, acc.shape[1]), jnp.float32)
         copies[0].wait()
         p = {z: gl[0, z - base] for z in own_planes}
         v = tuple({z: gl[1 + f, z - base] for z in own_planes} for f in range(3))
@@ -322,13 +323,16 @@
         store_flow(senders[("guess", 0)], v)
         copies[3].wait()
 
-        def gram_step(i, total):
-            t = jnp.swapaxes(basis[:, i], 0, 1)
+        def thirds(t, axis):
             hi = t.astype(jnp.bfloat16)
             rest = t - hi.astype(jnp.float32)
             mid = rest.astype(jnp.bfloat16)
             low = (rest - mid.astype(jnp.float32)).astype(jnp.bfloat16)
-            parts = jnp.concatenate([hi, mid, low], axis=1)
+            return jnp.concatenate([hi, mid, low], axis=axis)
+
+        def gram_step(i, total):
+            t = jnp.swapaxes(basis[:, i], 0, 1)
+            parts = thirds(t, 1)
             flat = jnp.concatenate([parts[j] for j in range(parts.shape[0])], axis=1)
             return total + lax.dot_general(
                 flat, flat, (((1,), (1,)), ((), ())), preferred_element_type=jnp.float32
@@ -394,11 +398,11 @@
                 acc[pl.ds(pl.multiple_of(8 * i, 8), 8), :] = jnp.sum(t, axis=1)
                 return carry
 
-            lax.fori_loop(0, rank // 8, coef_step, 0)
-            ones = jnp.ones((8, acc.shape[1]), jnp.float32)
+            lax.fori_loop(0, rank // 8, coef_step, 0, unroll=2)
+            parts = thirds(acc[...], 1)
+            ones = jnp.ones((8, parts.shape[1]), jnp.bfloat16)
             cf[index, s] = lax.dot_general(
-                ones, acc[...], (((1,), (1,)), ((), ())),
-                precision=lax.Precision.HIGHEST, preferred_element_type=jnp.float32,
+                ones, parts, (((1,), (1,)), ((), ())), preferred_element_type=jnp.float32
             )
             line = pl.ds(0, 1)
             return [
@@ -472,8 +476,8 @@
                     m = jnp.where(rows == j + i, part[i][:1], m)
             return m
 
-        width = 4 if rank % 4 == 0 else 1
-        half = rank // 2 // width * width
+        width = 8 if rank % 8 == 0 else 1
+        half = rank * 3 // 4 // width * width
         m = eliminate(m, 0, half)
         wait(moved)
         wait(moved_flow)
@@ -608,6 +612,11 @@
     return kernel, reach_max, n_wins, n_sent
 
 
+def hand_over(states_in, coords_in, states_out, coords_out):
+    states_out[...] = states_in[...]
+    coords_out[...] = coords_in[...]
+
+
 def solution(mesh):
     n_tm, n_sp = mesh.shape["tm"], mesh.shape["space"]
 
@@ -618,7 +627,7 @@
         dma = pltpu.SemaphoreType.DMA
         kernel, reach, n_wins, n_sent = make_kernel(n_tm, n_sp, rank, slab, nx, ny)
         wide = slab + 2 * reach
-        return pl.pallas_call(
+        made = pl.pallas_call(
             kernel,
             out_shape=(
                 jax.ShapeDtypeStruct((4, 4, slab, nx, ny), f32),
@@ -651,6 +660,12 @@
                 collective_id=0, has_side_effects=True, vmem_limit_bytes=60 * 1024 * 1024
             ),
         )(speed[None], forcing, guess[0], basis[0].reshape(rank, 4 * slab, nx, ny))
+        return pl.pallas_call(
+            hand_over,
+            out_shape=[jax.ShapeDtypeStruct(a.shape, f32) for a in made],
+            in_specs=[pl.BlockSpec(memory_space=pltpu.VMEM)] * 2,
+            out_specs=[pl.BlockSpec(memory_space=pltpu.VMEM)] * 2,
+        )(*made)
 
     placed = (
         P("space", None, None),

time: 64.1 us -> 61.4 us (0.958)
  local copies, waits for them, and re-layouts: 2.8 us -> 0 us
    unnamed x2 -> x0, local copies, waits for them, and re-layouts: 2.8 us -> none
    pallas_call x0 -> x1, Pallas kernels: none -> 1.68 us  [body(): pl.pallas_call(hand_over, out_shape=[jax.ShapeDtypeStruct(a.shape, f32) f...]
    pallas_call x1, Pallas kernels: 60.4 us -> 58.9 us  [body(): pl.pallas_call(kernel, out_shape=(jax.ShapeDtypeStruct((4, 4, slab, nx, n...]
where the time goes in v3:
time: 61.4 us; the launch traced here: 61.3 us
  Pallas kernels  60.6 us (99%)
  between operations  0.64 us (1%)
    pallas_call x1, Pallas kernels, body(): pl.pallas_call(kernel, out_shape=(jax.ShapeDtypeStruct((4, 4, slab, nx, n...  58.9 us
    pallas_call x1, Pallas kernels, body(): pl.pallas_call(hand_over, out_shape=[jax.ShapeDtypeStruct(a.shape, f32) f...  1.68 us

profile of v3, /device:TPU:0, one launch (start us, length us, event | category | flops | bytes accessed | tf_op | source)
XLA Modules:
  0.0 61.3 jit_solution(13237905247720976892)
XLA Ops:
  0.6 58.9 %shard_map.59 = (f32[4,4,2,16,128]{4,3,2,1,0:T(8,128)}, f32[1,64]{1,0:T(1,128)}) custom-call(f32[1,2,16,128]{3,2,1,0:T(8,128)} %bitcast.5, f32[4,2,16,128]{3,2,1,0:T(8,128)} %forcing_in.1, f32[4,2,16,128]{3,2,1,0:T(8,128)} %bitcast.4, f32[64,8,16,128]{3,2,1,0:T(8,128)} %bitcast.3), custom_call_target="tpu_custom_call" | custom-call | tf_op jit(solution)/shard_map/pallas_call | solution.py:630
  59.6 1.7 %shard_map.60 = (f32[4,4,2,16,128]{4,3,2,1,0:T(8,128)}, f32[1,64]{1,0:T(1,128)}) custom-call(f32[4,4,2,16,128]{4,3,2,1,0:T(8,128)} %get-tuple-element.4.states_in, f32[1,64]{1,0:T(1,128)} %get-tuple-element.5.coords_in), custom_call_target="tpu_custom_call" | custom-call | tf_op jit(solution)/shard_map/pallas_call | solution.py:663

commit v4 on v3

--- a/solution.py
+++ b/solution.py
@@ -480,11 +480,11 @@
         half = rank * 3 // 4 // width * width
         m = eliminate(m, 0, half)
         wait(moved)
-        wait(moved_flow)
         p, d = load_window(wins[("relaxed", 0)][0], 4)
         p, d, total = evolve(p, d, 4, DT, loads)
+        store_wave(tb.at[0], p, d)
+        wait(moved_flow)
         v = push(load_flow(wins[("relaxed", 0)][0]), total, DT)
-        store_wave(tb.at[0], p, d)
         store_flow(tb.at[0], v)
         x = each(minus, (p, v, d), load_state(rel))
 
@@ -532,28 +532,33 @@
             ))
         carry = None
         for j in range(n_chain, 0, -1):
-            wait(chains[j - 1])
+            wait(chains[j - 1][:-1])
             ref = wins[("gap", j)][0]
             used = before >= GROUP * j
             q, d = load_window(ref, 2 * j)
-            u = load_flow(ref)
 
             def kept(planes):
                 return {z: jnp.where(used, planes[z], 0.0) for z in planes}
 
-            q, d, u = kept(q), kept(d), tuple(kept(a) for a in u)
+            q, d = kept(q), kept(d)
             if carry is not None:
                 q = {z: q[z] + carry[0][z] for z in q}
                 d = {z: d[z] + carry[1][z] for z in d}
-                u = tuple({z: u[f][z] + carry[2][f][z] for z in own_planes} for f in range(3))
+            before_steps = []
             for step in range(2):
                 reach = 2 * j - 1 - step
-                u = push(u, q, 8 * DT)
+                before_steps.append(q)
                 nq, nd = {}, {}
                 for z in range(base - reach, base + slab + reach):
                     nd[z] = d[z] - 8 * DT * lap(q, z)
                     nq[z] = q[z] - scale(z, 8 * DT) * nd[z]
                 q, d = nq, nd
+            wait(chains[j - 1][-1:])
+            u = tuple(kept(a) for a in load_flow(ref))
+            if carry is not None:
+                u = tuple({z: u[f][z] + carry[2][f][z] for z in own_planes} for f in range(3))
+            for planes in before_steps:
+                u = push(u, planes, 8 * DT)
             carry = (q, d, u)
         if carry is not None:
             x = each(plus, x, (carry[0], carry[2], carry[1]))

time: 61.4 us -> 61.4 us (level)
  no operation moved by 1% of the time
where the time goes in v4:
time: 61.4 us; the launch traced here: 61.3 us
  Pallas kernels  60.6 us (99%)
  between operations  0.64 us (1%)
    pallas_call x1, Pallas kernels, body(): pl.pallas_call(kernel, out_shape=(jax.ShapeDtypeStruct((4, 4, slab, nx, n...  59 us
    pallas_call x1, Pallas kernels, body(): pl.pallas_call(hand_over, out_shape=[jax.ShapeDtypeStruct(a.shape, f32) f...  1.68 us

profile of v4, /device:TPU:0, one launch (start us, length us, event | category | flops | bytes accessed | tf_op | source)
XLA Modules:
  0.0 61.3 jit_solution(7740448673656277601)
XLA Ops:
  0.6 59.0 %shard_map.59 = (f32[4,4,2,16,128]{4,3,2,1,0:T(8,128)}, f32[1,64]{1,0:T(1,128)}) custom-call(f32[1,2,16,128]{3,2,1,0:T(8,128)} %bitcast.5, f32[4,2,16,128]{3,2,1,0:T(8,128)} %forcing_in.1, f32[4,2,16,128]{3,2,1,0:T(8,128)} %bitcast.4, f32[64,8,16,128]{3,2,1,0:T(8,128)} %bitcast.3), custom_call_target="tpu_custom_call" | custom-call | tf_op jit(solution)/shard_map/pallas_call | solution.py:635
  59.6 1.7 %shard_map.60 = (f32[4,4,2,16,128]{4,3,2,1,0:T(8,128)}, f32[1,64]{1,0:T(1,128)}) custom-call(f32[4,4,2,16,128]{4,3,2,1,0:T(8,128)} %get-tuple-element.4.states_in, f32[1,64]{1,0:T(1,128)} %get-tuple-element.5.coords_in), custom_call_target="tpu_custom_call" | custom-call | tf_op jit(solution)/shard_map/pallas_call | solution.py:668
